TPU v7x, 32 devices: a whole 2x2x4 slice. The times are simulated.
32 devices in a mesh: gx: 8 (over y, x, core), gy: 4 (over z).
Axes of the slice: x: 2, y: 2, z: 4, core: 2. Of those that a mesh axis runs over, the one named last changes fastest.
Arguments:
- coefficients: float32 [2, 2048, 512], P(None, 'gx', 'gy'), may hold values from -0.125 to 0.125
- spacing: float32 [31], replicated, may hold values from 0.6 to 1.5
Outputs:
- zcoord: float32 [32, 4096, 512], P(None, 'gx', 'gy')
- slopes: float32 [2, 32, 4096, 512], P(None, None, 'gx', 'gy')
- jacobian: float32 [32, 4096, 512], P(None, 'gx', 'gy')
- quality: float32 [32, 4096, 512], P(None, 'gx', 'gy')
All inputs are finite; a program needn't handle non-finite values.
Results may differ from a plain program's by a relative error of at most 0.0003.
Values sent between devices are 32-bit elements; how exact they have to be, the bound alone decides.
A program may use at most 128 MiB of HBM per device.

v0:
```python
import functools
import math

import jax
import jax.numpy as jnp
import numpy as np
from jax import lax
from jax.experimental import pallas as pl
from jax.experimental.pallas import tpu as pltpu
from jax.sharding import PartitionSpec as P

NX = 4096


BOUNDARY = (
    (-24.0 / 17.0, 59.0 / 34.0, -4.0 / 17.0, -3.0 / 34.0, 0.0, 0.0),
    (-0.5, 0.0, 0.5, 0.0, 0.0, 0.0),
    (4.0 / 43.0, -59.0 / 86.0, 0.0, 59.0 / 86.0, -4.0 / 43.0, 0.0),
    (3.0 / 98.0, 0.0, -59.0 / 98.0, 0.0, 32.0 / 49.0, -4.0 / 49.0),
)
TOPO_SCALE = 0.1


def extended(cells, sides, width):
    for axis, dim in sides:
        count = lax.axis_size(axis)
        head = lax.slice_in_dim(cells, 0, width, axis=dim)
        tail = lax.slice_in_dim(cells, cells.shape[dim] - width, cells.shape[dim], axis=dim)
        cells = jnp.concatenate(
            [
                lax.ppermute(tail, axis, [(i, (i + 1) % count) for i in range(count)]),
                cells,
                lax.ppermute(head, axis, [((i + 1) % count, i) for i in range(count)]),
            ],
            axis=dim,
        )
    return cells


def vertical(field):
    levels = field.shape[0]
    top_rows = []
    bottom_rows = []
    for row_id in range(4):
        upper = None
        lower = None
        for level_id, factor in enumerate(BOUNDARY[row_id]):
            if factor != 0.0:
                term_up = factor * field[level_id]
                term_down = -factor * field[levels - 1 - level_id]
                upper = term_up if upper is None else upper + term_up
                lower = term_down if lower is None else lower + term_down
        top_rows.append(upper)
        bottom_rows.append(lower)
    inner = (
        8.0 * (field[5 : levels - 3] - field[3 : levels - 5])
        - (field[6 : levels - 2] - field[2 : levels - 6])
    ) / 12.0
    return jnp.concatenate([jnp.stack(top_rows), inner, jnp.stack(bottom_rows[::-1])], axis=0)


def stretching(spacing):
    summed = jnp.sum(spacing)
    return jnp.concatenate([jnp.zeros((1,), spacing.dtype), jnp.cumsum(spacing)]) / summed


def column_depth(surface, stretch):
    levels = stretch.shape[0]
    return (levels - 1.0) * (surface[None] + (1.0 - surface[None]) * stretch[:, None, None])


def basis(count, x_cells):
    mode_ids = jnp.arange(count, dtype=jnp.int32)
    phase = (mode_ids[:, None] * x_cells[None, :] % NX).astype(jnp.float32) * (2.0 * math.pi / NX)
    return (jnp.cos(phase), jnp.sin(phase))


def project(cosine, sine, portion):
    first = jnp.dot(
        cosine.T, portion[0], precision=lax.Precision.HIGHEST, preferred_element_type=jnp.float32
    )
    return first + jnp.dot(
        sine.T, portion[1], precision=lax.Precision.HIGHEST, preferred_element_type=jnp.float32
    )


LANES = 128
RADIX = 16
TILE = 8
MESH = pl.DeviceIdType.MESH


def level_weights(gaps):
    levels = gaps + 1
    summed = np.tril(np.ones((levels, gaps)), -1)
    deriv = np.zeros((levels, levels))
    for row in range(levels):
        if row < 4:
            deriv[row, :6] = BOUNDARY[row]
        elif row >= levels - 4:
            deriv[row, ::-1][:6] = -np.array(BOUNDARY[levels - 1 - row])
        else:
            deriv[row, row - 2 : row + 3] = np.array([1.0, -8.0, 0.0, 8.0, -1.0]) / 12.0
    return np.stack([summed, deriv @ summed]).astype(np.float32)


def transform_tables(modes, groups):
    part = NX // RADIX
    own = part // groups
    block = own + TILE
    rows = []
    for dest in range(groups):
        first = dest * own
        rows += list(range(first, first + own)) + [first - 1, first + own] + [first] * (TILE - 2)
    angle = 2.0 * np.pi / part * ((np.array(rows)[:, None] * np.arange(part)[None]) % part)
    full = np.concatenate([np.cos(angle), np.sin(angle)], axis=1).astype(np.float32)
    turn = 2.0 * np.pi / NX * (np.arange(RADIX)[:, None] * np.arange(part)[None])
    twiddle = np.concatenate([np.cos(turn), np.sin(turn)], axis=1).astype(np.float32)
    return full, twiddle, block


def rotate(value, angle):
    re, im = value
    cos, sin = math.cos(angle), math.sin(angle)
    if abs(sin) < 1e-12:
        return (re, im) if cos > 0 else (-re, -im)
    if abs(cos) < 1e-12:
        return (im, -re) if sin > 0 else (-im, re)
    if abs(abs(cos) - abs(sin)) < 1e-12:
        unit = math.sqrt(0.5)
        a, b = math.copysign(1.0, cos), math.copysign(1.0, sin)
        one = re * unit if a > 0 else re * -unit
        two = im * unit if a > 0 else im * -unit
        if a == b:
            return one + two, two - one
        return one - two, two + one
    return re * cos + im * sin, im * cos - re * sin


def fourier(values):
    count = len(values)
    if count == 1:
        return values
    even, odd = fourier(values[0::2]), fourier(values[1::2])
    out = [None] * count
    for i in range(count // 2):
        re, im = rotate(odd[i], 2.0 * math.pi * i / count)
        out[i] = (even[i][0] + re, even[i][1] + im)
        out[i + count // 2] = (even[i][0] - re, even[i][1] - im)
    return out


def split(value):
    high = value.astype(jnp.bfloat16)
    return high, (value - high.astype(jnp.float32)).astype(jnp.bfloat16)


def regroup(values, lane, width):
    values = list(values)
    step = len(values) // 2
    while step:
        upper = (lane // width) & step != 0
        shift = step * width
        for i in range(len(values)):
            if not i & step:
                low, high = values[i], values[i + step]
                values[i] = jnp.where(upper, pltpu.roll(high, shift, 1), low)
                values[i + step] = jnp.where(upper, high, pltpu.roll(low, LANES - shift, 1))
        step //= 2
    return values


def surface_kernel(
    groups, columns, coef, spacing, weights, basis_high_hbm, basis_low_hbm, twiddle,
    s_out, dx_out, dy_out, table,
    basis_high, basis_low, turned, gathered, high, low, product, landed, above, below,
    extended_s, outer, best, bests, edges, edge_product,
    const_sem, send_one, recv_one, send_two, recv_two, send_side, recv_side, send_max, recv_max,
):
    gx, gy = lax.axis_index("gx"), lax.axis_index("gy")

    def moved_by(d):
        return lax.rem(gx + d // columns, groups), lax.rem(gy + d % columns, columns)

    loads = [
        pltpu.make_async_copy(basis_high_hbm, basis_high, const_sem.at[0]),
        pltpu.make_async_copy(basis_low_hbm, basis_low, const_sem.at[1]),
    ]
    for load in loads:
        load.start()
    barrier = pltpu.get_barrier_semaphore()
    for d in range(1, groups * columns):
        pl.semaphore_signal(barrier, inc=1, device_id=moved_by(d), device_id_type=MESH)

    part = coef.shape[1]
    ys = coef.shape[2] // groups
    turned[:, :part] = coef[0].T
    turned[:, part:] = coef[1].T
    pl.semaphore_wait(barrier, groups * columns - 1)

    first = []
    for d in range(1, groups):
        target = lax.rem(gx + d, groups)
        copy = pltpu.make_async_remote_copy(
            src_ref=turned.at[pl.ds(pl.multiple_of(target * ys, TILE), ys)],
            dst_ref=gathered.at[gx],
            send_sem=send_one.at[d],
            recv_sem=recv_one.at[d],
            device_id=(target, gy),
            device_id_type=MESH,
        )
        copy.start()
        first.append(copy)
    gathered[gx] = turned[pl.ds(pl.multiple_of(gx * ys, TILE), ys), :]

    thick = spacing[...]
    total = jnp.sum(thick, axis=1, keepdims=True)
    scale = spacing.shape[1] * 1.0
    levels = spacing.shape[1] + 1
    stretch = jnp.sum(weights[0] * thick, axis=1, keepdims=True) / total
    slope = jnp.sum(weights[1] * thick, axis=1, keepdims=True) / total
    least = jnp.min(slope, axis=0, keepdims=True)
    table[0] = jnp.broadcast_to(scale * stretch, (levels, LANES))
    table[1] = jnp.broadcast_to(scale * (1.0 - stretch), (levels, LANES))
    table[2] = jnp.broadcast_to(scale * slope, (levels, LANES))

    for copy in first:
        copy.wait()

    half = NX // RADIX
    parts = half // part
    values = []
    for i in range(RADIX // 2):
        re = [gathered[i * parts + p, :, :part] for p in range(parts)]
        im = [gathered[i * parts + p, :, part:] for p in range(parts)]
        values.append(
            (re[0], im[0]) if parts == 1 else (jnp.concatenate(re, 1), jnp.concatenate(im, 1))
        )
    even = fourier(values)
    odd = fourier([rotate(v, 2.0 * math.pi * i / RADIX) for i, v in enumerate(values)])
    for r in range(RADIX):
        re, im = (even if r % 2 == 0 else odd)[r // 2]
        if r:
            cos, sin = twiddle[r : r + 1, :half], twiddle[r : r + 1, half:]
            re, im = re * cos + im * sin, im * cos - re * sin
        rows = slice(r * ys, (r + 1) * ys)
        high[rows, :half], low[rows, :half] = split(re)
        high[rows, half:], low[rows, half:] = split(im)
        rows = slice(r * TILE, (r + 1) * TILE)
        edges[rows, :half] = jnp.where(gx == 0, re[:TILE], re[ys - TILE :])
        edges[rows, half:] = jnp.where(gx == 0, im[:TILE], im[ys - TILE :])

    for load in loads:
        load.wait()
    dot = functools.partial(
        lax.dot_general,
        dimension_numbers=(((1,), (1,)), ((), ())),
        preferred_element_type=jnp.float32,
    )
    raw = dot(basis_high[...], high[...])
    raw = raw + dot(basis_high[...], low[...])
    raw = raw + dot(basis_low[...], high[...])
    best[...] = jnp.broadcast_to(jnp.max(raw, keepdims=True), (TILE, LANES))
    maxima = []
    for d in range(1, groups * columns):
        copy = pltpu.make_async_remote_copy(
            src_ref=best,
            dst_ref=bests.at[d],
            send_sem=send_max.at[d],
            recv_sem=recv_max.at[d],
            device_id=moved_by(d),
            device_id_type=MESH,
        )
        copy.start()
        maxima.append(copy)
    block = basis_high.shape[0] // groups
    own = block - TILE
    sublane = lax.broadcasted_iota(jnp.int32, (TILE, LANES), 0)
    for dest in range(groups):
        rows = raw[dest * block : (dest + 1) * block]
        product[dest, :own] = rows[:own, :LANES]
        product[dest, own : 2 * own] = rows[:own, LANES:]
        product[dest, 2 * own :] = jnp.where(sublane == 0, rows[own:, LANES:], rows[own:, :LANES])

    second = []
    for d in range(1, groups):
        target = lax.rem(gx + d, groups)
        copy = pltpu.make_async_remote_copy(
            src_ref=product.at[target],
            dst_ref=landed.at[gx],
            send_sem=send_two.at[d],
            recv_sem=recv_two.at[d],
            device_id=(target, gy),
            device_id_type=MESH,
        )
        copy.start()
        second.append(copy)
    landed[gx] = product[gx]

    edge_high, edge_low = split(edges[...])
    raw = dot(basis_high[...], edge_high)
    raw = raw + dot(basis_high[...], edge_low)
    raw = raw + dot(basis_low[...], edge_high)
    for dest in range(groups):
        edge_product[dest] = raw[dest * block : dest * block + own]

    def side_copy(which, dest):
        return pltpu.make_async_remote_copy(
            src_ref=edge_product.at[dest],
            dst_ref=(above, below)[which],
            send_sem=send_side.at[dest],
            recv_sem=recv_side.at[which],
            device_id=(dest, lax.rem(gy + (columns - 1, 1)[which], columns)),
            device_id_type=MESH,
        )

    for which, sender in enumerate((0, groups - 1)):

        @pl.when(gx == sender)
        def _():
            for dest in range(groups):
                side_copy(which, dest).start()

    for copy in second:
        copy.wait()

    count = own * RADIX
    lane = lax.broadcasted_iota(jnp.int32, (own, LANES), 1)
    for part_id in range(RADIX // groups):
        rows = slice(part_id * own, (part_id + 1) * own)
        pieces = regroup([landed[j, rows, :] for j in range(groups)], lane, ys)
        for i, piece in enumerate(pieces):
            r = part_id * groups + i
            extended_s[pl.ds(TILE + r, own, stride=RADIX), :] = TOPO_SCALE * jnp.tanh(piece * 0.25)
    lane = lax.broadcasted_iota(jnp.int32, (TILE, LANES), 1)
    pieces = regroup([landed[j, 2 * own :, :] for j in range(groups)], lane, ys)
    for i in range(2):
        before = TOPO_SCALE * jnp.tanh(pieces[groups - 2 + i] * 0.25)
        after = TOPO_SCALE * jnp.tanh(pieces[i] * 0.25)
        extended_s[TILE - 2 + i : TILE - 1 + i, :] = before[0:1]
        extended_s[TILE + count + i : TILE + count + i + 1, :] = after[1:2]
    s_out[...] = extended_s[TILE : TILE + count, :]
    dx_out[...] = (
        8.0 * (extended_s[TILE + 1 : TILE + 1 + count, :] - extended_s[TILE - 1 : TILE - 1 + count, :])
        - (extended_s[TILE + 2 : TILE + 2 + count, :] - extended_s[TILE - 2 : TILE - 2 + count, :])
    ) * (1.0 / 12.0)

    for which, sender in enumerate((0, groups - 1)):
        side_copy(which, 0).wait_recv()

        @pl.when(gx == sender)
        def _():
            for dest in range(groups):
                side_copy(which, dest).wait_send()

    lane = lax.broadcasted_iota(jnp.int32, (own, LANES), 1)
    right_all = TOPO_SCALE * jnp.tanh(above[...] * 0.25)
    left_all = TOPO_SCALE * jnp.tanh(below[...] * 0.25)
    for r in range(RADIX):
        right = pltpu.roll(right_all, LANES - r * TILE, 1) if r else right_all
        left = pltpu.roll(left_all, LANES - TILE - r * TILE, 1) if r != RADIX - 1 else left_all
        outer[pl.ds(r, own, stride=RADIX), :] = jnp.where(lane < LANES // 2, right, left)
    inner, edge = s_out[...], outer[...]
    lane = lax.broadcasted_iota(jnp.int32, (count, LANES), 1)

    def moved(by):
        taken = lane < by if by > 0 else lane >= LANES + by
        return pltpu.roll(jnp.where(taken, edge, inner), (LANES - by) % LANES, 1)

    dy_out[...] = (8.0 * (moved(1) - moved(-1)) - (moved(2) - moved(-2))) * (1.0 / 12.0)

    for copy in maxima:
        copy.wait()
    peak = best[0:1, :]
    for d in range(1, groups * columns):
        peak = jnp.maximum(peak, bests[d, 0:1, :])
    peak = TOPO_SCALE * jnp.tanh(peak * 0.25)
    table[3] = jnp.broadcast_to(slope, (levels, LANES)) / ((1.0 - peak) * least)


def surface_by_kernel(coefficients, spacing, groups, columns):
    _, modes, ys = coefficients.shape
    full, twiddle, block = transform_tables(modes * groups, groups)
    high = full.astype(jnp.bfloat16)
    low = (full - high.astype(np.float32)).astype(jnp.bfloat16)
    weights = level_weights(spacing.shape[0])
    levels = spacing.shape[0] + 1
    count = NX // groups
    part = NX // RADIX
    width = RADIX * (ys // groups)
    own = block - TILE
    vmem = pl.BlockSpec(memory_space=pltpu.VMEM)
    hbm = pl.BlockSpec(memory_space=pl.ANY)
    plane = jax.ShapeDtypeStruct((count, ys), jnp.float32)
    dma = pltpu.SemaphoreType.DMA
    return pl.pallas_call(
        functools.partial(surface_kernel, groups, columns),
        out_shape=(plane, plane, plane, jax.ShapeDtypeStruct((4, levels, LANES), jnp.float32)),
        in_specs=[vmem, vmem, vmem, hbm, hbm, vmem],
        out_specs=(vmem,) * 4,
        scratch_shapes=[
            pltpu.VMEM(full.shape, jnp.bfloat16),
            pltpu.VMEM(full.shape, jnp.bfloat16),
            pltpu.VMEM((ys, 2 * modes), jnp.float32),
            pltpu.VMEM((groups, ys // groups, 2 * modes), jnp.float32),
            pltpu.VMEM((width, 2 * part), jnp.bfloat16),
            pltpu.VMEM((width, 2 * part), jnp.bfloat16),
            pltpu.VMEM((groups, 2 * own + TILE, LANES), jnp.float32),
            pltpu.VMEM((groups, 2 * own + TILE, LANES), jnp.float32),
            pltpu.VMEM((own, LANES), jnp.float32),
            pltpu.VMEM((own, LANES), jnp.float32),
            pltpu.VMEM((count + 2 * TILE, ys), jnp.float32),
            pltpu.VMEM((count, ys), jnp.float32),
            pltpu.VMEM((TILE, LANES), jnp.float32),
            pltpu.VMEM((groups * columns, TILE, LANES), jnp.float32),
            pltpu.VMEM((RADIX * TILE, 2 * part), jnp.float32),
            pltpu.VMEM((groups, own, LANES), jnp.float32),
            dma((2,)),
            dma((groups,)),
            dma((groups,)),
            dma((groups,)),
            dma((groups,)),
            dma((groups,)),
            dma((2,)),
            dma((groups * columns,)),
            dma((groups * columns,)),
        ],
        compiler_params=pltpu.CompilerParams(collective_id=0, has_side_effects=True),
    )(coefficients, spacing[None], jnp.asarray(weights), jnp.asarray(high), jnp.asarray(low), jnp.asarray(twiddle))


def surface_by_gather(coefficients, spacing, groups):
    x_count = NX // groups
    x_first = lax.axis_index("gx") * x_count
    x_cells = x_first + jnp.arange(x_count, dtype=jnp.int32)
    portion = lax.all_gather(coefficients, "gx", axis=1, tiled=True)
    cosine, sine = basis(portion.shape[1], x_cells)
    surface = TOPO_SCALE * jnp.tanh(project(cosine, sine, portion) * 0.25)
    stretch = stretching(spacing)
    scale = stretch.shape[0] - 1.0
    slope = vertical(stretch)
    peak = lax.pmax(jnp.max(surface), ("gx", "gy"))
    wide = extended(surface, (("gx", 0), ("gy", 1)), 2)
    dx = (8.0 * (wide[3:-1] - wide[1:-3]) - (wide[4:] - wide[:-4]))[:, 2:-2] / 12.0
    dy = (8.0 * (wide[:, 3:-1] - wide[:, 1:-3]) - (wide[:, 4:] - wide[:, :-4]))[2:-2] / 12.0
    rows = [scale * stretch, scale * (1.0 - stretch), scale * slope]
    rows.append(slope / ((1.0 - peak) * jnp.min(slope)))
    table = jnp.broadcast_to(jnp.stack(rows)[:, :, None], (4, stretch.shape[0], LANES))
    return surface, dx, dy, table


def levels_kernel(depth, s_ref, dx_ref, dy_ref, table, z_ref, slopes_ref, jac_ref, quality_ref):
    first = pl.program_id(0) * depth

    def row(which, level):
        return table[which, pl.ds(first + level, 1), :]

    for level in range(depth):
        s, gain = s_ref[...], row(1, level)
        z_ref[level] = row(0, level) + gain * s
        slopes_ref[0, level] = gain * dx_ref[...]
        slopes_ref[1, level] = gain * dy_ref[...]
        rest = 1.0 - s
        jac_ref[level] = row(2, level) * rest
        quality_ref[level] = row(3, level) * rest


def all_levels(s, dx, dy, table):
    levels = table.shape[1]
    rows, columns = s.shape
    depth = 2
    plane = pl.BlockSpec((rows, columns), lambda i: (0, 0))
    field = pl.BlockSpec((depth, rows, columns), lambda i: (i, 0, 0))
    shape = jax.ShapeDtypeStruct((levels, rows, columns), jnp.float32)
    return pl.pallas_call(
        functools.partial(levels_kernel, depth),
        grid=(levels // depth,),
        in_specs=[plane, plane, plane, pl.BlockSpec(table.shape, lambda i: (0, 0, 0))],
        out_specs=(
            field,
            pl.BlockSpec((2, depth, rows, columns), lambda i: (0, i, 0, 0)),
            field,
            field,
        ),
        out_shape=(
            shape,
            jax.ShapeDtypeStruct((2, levels, rows, columns), jnp.float32),
            shape,
            shape,
        ),
    )(s, dx, dy, table)


def shards(coefficients, spacing):
    groups, columns = lax.axis_size("gx"), lax.axis_size("gy")
    _, modes, ys = coefficients.shape
    fits = (
        ys == LANES
        and modes % LANES == 0
        and modes * groups * 2 == NX
        and ys % (groups * RADIX) == 0
        and ys == groups * RADIX
        and groups * TILE * 2 == RADIX * TILE
        and (NX // RADIX) % (groups * TILE) == 0
        and columns > 1
    )
    if fits:
        parts = surface_by_kernel(coefficients, spacing, groups, columns)
    else:
        parts = surface_by_gather(coefficients, spacing, groups)
    return all_levels(*parts)


def solution(mesh):
    return jax.shard_map(
        shards,
        mesh=mesh,
        in_specs=(P(None, "gx", "gy"), P()),
        out_specs=(
            P(None, "gx", "gy"),
            P(None, None, "gx", "gy"),
            P(None, "gx", "gy"),
            P(None, "gx", "gy"),
        ),
        check_vma=False,
    )
```

profile of v0, /device:TPU:0, one launch (start us, length us, event | category | flops | bytes accessed | tf_op | source)
XLA Modules:
  0.0 38.1 jit_solution(14844222767014426257)
XLA Ops:
  0.6 22.9 %shard_map.93 = (f32[512,128]{1,0:T(8,128)}, f32[512,128]{1,0:T(8,128)}, f32[512,128]{1,0:T(8,128)}, f32[4,32,128]{2,1,0:T(8,128)}) custom-call(f32[2,256,128]{2,1,0:T(8,128)} %coef.1, f32[1,31]{1,0:T(1,128)} %bitcast.1, f32[2,32,31]{2,1,0:T(8,128)} %constant.8.clone.weights, bf16[320,512]{1,0:T(8,128)(2,1)} %constant.9.clone.basis_high_hbm, ...), custom_call_target="tpu_custom_call" | custom-call | tf_op jit(solution)/shard_map/pallas_call | solution.py:396
  23.5 14.6 %shard_map.94 = (f32[32,512,128]{2,1,0:T(8,128)}, f32[2,32,512,128]{3,2,1,0:T(8,128)}, f32[32,512,128]{2,1,0:T(8,128)}, f32[32,512,128]{2,1,0:T(8,128)}) custom-call(f32[512,128]{1,0:T(8,128)} %get-tuple-element.8.s_ref, f32[512,128]{1,0:T(8,128)} %get-tuple-element.9.dx_ref, f32[512,128]{1,0:T(8,128)} %get-tuple-element.10.dy_ref, ...), custom_call_target="tpu_custom_call" | custom-call | tf_op jit(solution)/shard_map/pallas_call | solution.py:475
where the time goes:
time: 38.4 us; the launch traced here: 38.1 us
  Pallas kernels  37.5 us (98%)
  between operations  0.64 us (2%)
    pallas_call x1, Pallas kernels, surface_by_kernel(): pl.pallas_call(functools.partial(surface_kernel, groups, columns), out_sh...  22.9 us
    pallas_call x1, Pallas kernels, all_levels(): pl.pallas_call(functools.partial(levels_kernel, depth), grid=(levels // d...  14.6 us

commit v1 on v0

v1 whole, which is shorter than its diff:
```python
import functools
import math

import jax
import jax.numpy as jnp
import numpy as np
from jax import lax
from jax.experimental import pallas as pl
from jax.experimental.pallas import tpu as pltpu
from jax.sharding import PartitionSpec as P

NX = 4096


BOUNDARY = (
    (-24.0 / 17.0, 59.0 / 34.0, -4.0 / 17.0, -3.0 / 34.0, 0.0, 0.0),
    (-0.5, 0.0, 0.5, 0.0, 0.0, 0.0),
    (4.0 / 43.0, -59.0 / 86.0, 0.0, 59.0 / 86.0, -4.0 / 43.0, 0.0),
    (3.0 / 98.0, 0.0, -59.0 / 98.0, 0.0, 32.0 / 49.0, -4.0 / 49.0),
)
TOPO_SCALE = 0.1


def extended(cells, sides, width):
    for axis, dim in sides:
        count = lax.axis_size(axis)
        head = lax.slice_in_dim(cells, 0, width, axis=dim)
        tail = lax.slice_in_dim(cells, cells.shape[dim] - width, cells.shape[dim], axis=dim)
        cells = jnp.concatenate(
            [
                lax.ppermute(tail, axis, [(i, (i + 1) % count) for i in range(count)]),
                cells,
                lax.ppermute(head, axis, [((i + 1) % count, i) for i in range(count)]),
            ],
            axis=dim,
        )
    return cells


def vertical(field):
    levels = field.shape[0]
    top_rows = []
    bottom_rows = []
    for row_id in range(4):
        upper = None
        lower = None
        for level_id, factor in enumerate(BOUNDARY[row_id]):
            if factor != 0.0:
                term_up = factor * field[level_id]
                term_down = -factor * field[levels - 1 - level_id]
                upper = term_up if upper is None else upper + term_up
                lower = term_down if lower is None else lower + term_down
        top_rows.append(upper)
        bottom_rows.append(lower)
    inner = (
        8.0 * (field[5 : levels - 3] - field[3 : levels - 5])
        - (field[6 : levels - 2] - field[2 : levels - 6])
    ) / 12.0
    return jnp.concatenate([jnp.stack(top_rows), inner, jnp.stack(bottom_rows[::-1])], axis=0)


def stretching(spacing):
    summed = jnp.sum(spacing)
    return jnp.concatenate([jnp.zeros((1,), spacing.dtype), jnp.cumsum(spacing)]) / summed


def column_depth(surface, stretch):
    levels = stretch.shape[0]
    return (levels - 1.0) * (surface[None] + (1.0 - surface[None]) * stretch[:, None, None])


def basis(count, x_cells):
    mode_ids = jnp.arange(count, dtype=jnp.int32)
    phase = (mode_ids[:, None] * x_cells[None, :] % NX).astype(jnp.float32) * (2.0 * math.pi / NX)
    return (jnp.cos(phase), jnp.sin(phase))


def project(cosine, sine, portion):
    first = jnp.dot(
        cosine.T, portion[0], precision=lax.Precision.HIGHEST, preferred_element_type=jnp.float32
    )
    return first + jnp.dot(
        sine.T, portion[1], precision=lax.Precision.HIGHEST, preferred_element_type=jnp.float32
    )


LANES = 128
RADIX = 16
TILE = 8
MESH = pl.DeviceIdType.MESH


def level_weights(gaps):
    levels = gaps + 1
    summed = np.tril(np.ones((levels, gaps)), -1)
    deriv = np.zeros((levels, levels))
    for row in range(levels):
        if row < 4:
            deriv[row, :6] = BOUNDARY[row]
        elif row >= levels - 4:
            deriv[row, ::-1][:6] = -np.array(BOUNDARY[levels - 1 - row])
        else:
            deriv[row, row - 2 : row + 3] = np.array([1.0, -8.0, 0.0, 8.0, -1.0]) / 12.0
    return np.stack([summed, deriv @ summed]).astype(np.float32)


def transform_tables(modes, groups):
    part = NX // RADIX
    own = part // groups
    block = own + TILE
    rows = []
    for dest in range(groups):
        first = dest * own
        rows += list(range(first, first + own)) + [first - 1, first + own] * (TILE // 2)
    angle = 2.0 * np.pi / part * ((np.array(rows)[:, None] * np.arange(part)[None]) % part)
    full = np.concatenate([np.cos(angle), np.sin(angle)], axis=1).astype(np.float32)
    turn = 2.0 * np.pi / NX * (np.arange(RADIX)[:, None] * np.arange(part)[None])
    twiddle = np.concatenate([np.cos(turn), np.sin(turn)], axis=1).astype(np.float32)
    return full, twiddle, block


def rotate(value, angle):
    re, im = value
    cos, sin = math.cos(angle), math.sin(angle)
    if abs(sin) < 1e-12:
        return (re, im) if cos > 0 else (-re, -im)
    if abs(cos) < 1e-12:
        return (im, -re) if sin > 0 else (-im, re)
    if abs(abs(cos) - abs(sin)) < 1e-12:
        unit = math.sqrt(0.5)
        a, b = math.copysign(1.0, cos), math.copysign(1.0, sin)
        one = re * unit if a > 0 else re * -unit
        two = im * unit if a > 0 else im * -unit
        if a == b:
            return one + two, two - one
        return one - two, two + one
    return re * cos + im * sin, im * cos - re * sin


def fourier(values):
    count = len(values)
    if count == 1:
        return values
    even, odd = fourier(values[0::2]), fourier(values[1::2])
    out = [None] * count
    for i in range(count // 2):
        re, im = rotate(odd[i], 2.0 * math.pi * i / count)
        out[i] = (even[i][0] + re, even[i][1] + im)
        out[i + count // 2] = (even[i][0] - re, even[i][1] - im)
    return out


def split(value):
    high = value.astype(jnp.bfloat16)
    return high, (value - high.astype(jnp.float32)).astype(jnp.bfloat16)


def butterfly(values, bit, lane):
    shift = bit * TILE
    upper = (lane // TILE) & bit != 0
    for i in sorted(values):
        if not i & bit and i | bit in values:
            low, high = values[i], values[i | bit]
            values[i] = jnp.where(upper, pltpu.roll(high, shift, 1), low)
            values[i | bit] = jnp.where(upper, high, pltpu.roll(low, LANES - shift, 1))
    return values


def blocks_of(chunk, groups):
    return [2 * j + (chunk + j // (groups // 2)) % 2 for j in range(groups)]


def arrived(view, sem):
    pltpu.make_async_copy(view, view, sem).wait()


def surface_kernel(
    groups, columns, coef_hbm, spacing_hbm, weights_hbm, basis_hbm, twiddle_hbm,
    s_out, sides, table,
    coef, spacing, weights, basis, twiddle, turned, gathered, operand,
    product_one, product_two, landed_one, landed_two, landed_sides, best, bests, partial,
    load_sem, send_one, recv_one, send_two, recv_two, send_side, recv_side,
    send_max, recv_max, later_sem,
):
    gx, gy = lax.axis_index("gx"), lax.axis_index("gy")
    cores, rows_of = 2, groups // 2

    def other(d):
        core = lax.rem(gx + d % cores, cores)
        row = lax.rem(gx // rows_of + d // rows_of, 2)
        col = lax.rem(gx // cores + (d // cores) % 2, 2)
        return row * rows_of + col * cores + core

    peers = [other(d) for d in (6, 7, 2, 3, 4, 5, 1)]
    loads = [
        pltpu.make_async_copy(src, dst, load_sem.at[i])
        for i, (src, dst) in enumerate((
            (coef_hbm, coef),
            (spacing_hbm, spacing),
            (weights_hbm, weights),
            (twiddle_hbm, twiddle),
            (basis_hbm, basis),
        ))
    ]
    for load in loads:
        load.start()

    barrier = pltpu.get_barrier_semaphore()
    for peer in peers:
        pl.semaphore_signal(barrier, inc=1, device_id=(peer, gy), device_id_type=MESH)
    for up in range(1, columns):

        @pl.when(gy + up < columns)
        def _():
            for d in range(groups):
                target = (lax.rem(gx + d, groups), gy + up)
                pl.semaphore_signal(barrier, inc=1, device_id=target, device_id_type=MESH)

    part = coef.shape[1]
    ys = coef.shape[2] // groups
    half = NX // RADIX
    flip = gx // rows_of

    def sub_of(chunk, target):
        return lax.rem(chunk + target // rows_of, 2)

    def turned_rows(chunk, target):
        return pl.ds(pl.multiple_of(target * ys + sub_of(chunk, target) * TILE, TILE), TILE)

    loads[0].wait()
    turned[:, :part] = coef[0].T
    turned[:, part:] = coef[1].T
    pl.semaphore_wait(barrier, groups - 1 + groups * gy)

    for chunk in range(2):
        for target in peers:
            pltpu.make_async_remote_copy(
                src_ref=turned.at[turned_rows(chunk, target)],
                dst_ref=gathered.at[chunk, gx],
                send_sem=send_one,
                recv_sem=recv_one.at[chunk],
                device_id=(target, gy),
                device_id_type=MESH,
            ).start()
    for down in range(1, columns):

        @pl.when(gy >= down)
        def _():
            for d in range(groups):
                target = (lax.rem(gx + d, groups), gy - down)
                pl.semaphore_signal(later_sem, inc=1, device_id=target, device_id_type=MESH)

    for chunk in range(2):
        gathered[chunk, gx] = turned[turned_rows(chunk, gx), :]

    for load in loads[1:]:
        load.wait()
    thick = spacing[...]
    total = jnp.sum(thick, axis=1, keepdims=True)
    scale = spacing.shape[1] * 1.0
    levels = spacing.shape[1] + 1
    stretch = jnp.sum(weights[0] * thick, axis=1, keepdims=True) / total
    slope = jnp.sum(weights[1] * thick, axis=1, keepdims=True) / total
    least = jnp.min(slope, axis=0, keepdims=True)
    table[0] = jnp.broadcast_to(scale * stretch, (levels, LANES))
    table[1] = jnp.broadcast_to(scale * (1.0 - stretch), (levels, LANES))
    table[2] = jnp.broadcast_to(scale * slope, (levels, LANES))

    rows = basis.shape[0] // 2
    block = rows // groups
    own = block - TILE
    count = own * RADIX
    width = RADIX * TILE
    dot = functools.partial(
        lax.dot_general,
        dimension_numbers=(((1,), (1,)), ((), ())),
        preferred_element_type=jnp.float32,
    )

    def transform(chunk):
        values = [
            (gathered[chunk, i, :, :part], gathered[chunk, i, :, part:]) for i in range(groups)
        ]
        even = fourier(values)
        odd = fourier([rotate(v, 2.0 * math.pi * i / RADIX) for i, v in enumerate(values)])
        for r in range(0, RADIX, 2):
            pair = []
            for k, (re, im) in ((r, even[r // 2]), (r + 1, odd[r // 2])):
                if k:
                    cos, sin = twiddle[k : k + 1, :half], twiddle[k : k + 1, half:]
                    re, im = re * cos + im * sin, im * cos - re * sin
                pair.append((re, im))
            for at, lanes in enumerate((slice(0, half), slice(half, 2 * half))):
                high, low = split(jnp.concatenate([pair[0][at], pair[1][at]], axis=0))
                operand[r * TILE : (r + 2) * TILE, lanes] = high
                operand[width + r * TILE : width + (r + 2) * TILE, lanes] = low
        both = dot(basis[:rows], operand[...])
        return both[:, :width] + both[:, width:] + dot(basis[rows:], operand[:width])

    def send_product(product, landed, chunk):
        for target in peers:
            pltpu.make_async_remote_copy(
                src_ref=product.at[target],
                dst_ref=landed.at[gx],
                send_sem=send_two,
                recv_sem=recv_two.at[chunk],
                device_id=(target, gy),
                device_id_type=MESH,
            ).start()
        landed[gx] = product[gx]

    def tallest(raw):
        return functools.reduce(jnp.maximum, [raw[i : i + TILE] for i in range(0, rows, TILE)])

    arrived(gathered.at[0, pl.ds(0, groups - 1)], recv_one.at[0])
    raw = transform(0)
    ends_one = [raw[dest * block + own : (dest + 1) * block] for dest in range(groups)]
    for dest in range(groups):
        product_one[dest] = raw[dest * block : dest * block + own]
    send_product(product_one, landed_one, 0)
    peak_one = tallest(raw)

    @pl.when(gy < columns - 1)
    def _():
        pl.semaphore_wait(later_sem, groups * (columns - 1 - gy))

    for which, sender in enumerate((0, groups - 1)):

        @pl.when(gx == sender)
        def _():
            for dest in range(groups):
                pltpu.make_async_remote_copy(
                    src_ref=product_one.at[dest],
                    dst_ref=landed_sides.at[which],
                    send_sem=send_side,
                    recv_sem=recv_side.at[which],
                    device_id=(dest, lax.rem(gy + (columns - 1, 1)[which], columns)),
                    device_id_type=MESH,
                ).start()

    arrived(gathered.at[1, pl.ds(0, groups - 1)], recv_one.at[1])
    raw = transform(1)
    sublane = lax.broadcasted_iota(jnp.int32, (TILE, LANES), 0)
    for dest in range(groups):
        product_two[dest, :own] = raw[dest * block : dest * block + own]
        product_two[dest, own:] = jnp.where(
            sublane < 2, ends_one[dest], raw[dest * block + own : (dest + 1) * block]
        )
    send_product(product_two, landed_two, 1)
    best[...] = jnp.broadcast_to(
        jnp.max(jnp.maximum(peak_one, tallest(raw)), keepdims=True), (TILE, LANES)
    )
    for d in range(1, groups * columns):
        pltpu.make_async_remote_copy(
            src_ref=best,
            dst_ref=bests.at[d],
            send_sem=send_max,
            recv_sem=recv_max,
            device_id=(
                lax.rem(gx + d // columns, groups),
                lax.rem(gy + d % columns, columns),
            ),
            device_id_type=MESH,
        ).start()

    def surface(piece):
        return TOPO_SCALE * jnp.tanh(piece * 0.25)

    lane = lax.broadcasted_iota(jnp.int32, (own, LANES), 1)
    arrived(landed_one.at[pl.ds(0, groups - 1)], recv_two.at[0])
    first = {b: surface(landed_one[j]) for j, b in enumerate(blocks_of(0, groups))}
    for bit in (2, 4):
        first = butterfly(first, bit, lane)
    for b, value in first.items():
        partial[b // 2] = value

    arrived(landed_two.at[pl.ds(0, groups - 1)], recv_two.at[1])
    second = {b: surface(landed_two[j, :own]) for j, b in enumerate(blocks_of(1, groups))}
    for bit in (2, 4):
        second = butterfly(second, bit, lane)
    pieces = {b: partial[b // 2] for b in first} | second
    for bit in (8, 1):
        pieces = butterfly(pieces, bit, lane)
    for r in range(RADIX):
        s_out[pl.ds(TILE + r, own, stride=RADIX), :] = pieces[r]

    lane = lax.broadcasted_iota(jnp.int32, (TILE, LANES), 1)
    ends = {b: surface(landed_two[b // 2, own:]) for b in range(2 * groups)}
    for bit in (2, 4, 8, 1):
        ends = butterfly(ends, bit, lane)
    is_late = lax.rem(lane // TILE + lane // (LANES // 2), 2)[0:1] == 1
    for i in range(2):
        before, after = ends[RADIX - 2 + i], ends[i]
        s_out[TILE - 2 + i : TILE - 1 + i, :] = jnp.where(is_late, before[2:3], before[0:1])
        s_out[TILE + count + i : TILE + count + i + 1, :] = jnp.where(
            is_late, after[3:4], after[1:2]
        )

    for which in range(2):
        arrived(landed_sides.at[which], recv_side.at[which])
        sides[which] = surface(landed_sides[which])

    arrived(turned.at[pl.ds(0, (groups - 1) * ys)], send_one)
    arrived(product_one.at[pl.ds(0, groups - 1)], send_two)
    arrived(product_two.at[pl.ds(0, groups - 1)], send_two)

    @pl.when(jnp.logical_or(gx == 0, gx == groups - 1))
    def _():
        arrived(product_one, send_side)

    arrived(bests.at[pl.ds(1, groups * columns - 1)], recv_max)
    arrived(bests.at[pl.ds(1, groups * columns - 1)], send_max)
    peak = best[0:1, :]
    for d in range(1, groups * columns):
        peak = jnp.maximum(peak, bests[d, 0:1, :])
    table[3] = jnp.broadcast_to(slope, (levels, LANES)) / ((1.0 - surface(peak)) * least)


def surface_by_kernel(coefficients, spacing, groups, columns):
    _, modes, ys = coefficients.shape
    full, twiddle, block = transform_tables(modes * groups, groups)
    high = full.astype(jnp.bfloat16)
    low = (full - high.astype(np.float32)).astype(jnp.bfloat16)
    basis = np.concatenate([high, low], axis=0)
    weights = level_weights(spacing.shape[0])
    levels = spacing.shape[0] + 1
    count = NX // groups
    own = block - TILE
    width = RADIX * TILE
    vmem = pl.BlockSpec(memory_space=pltpu.VMEM)
    hbm = pl.BlockSpec(memory_space=pltpu.HBM)
    dma = pltpu.SemaphoreType.DMA
    f32 = jnp.float32
    return pl.pallas_call(
        functools.partial(surface_kernel, groups, columns),
        out_shape=(
            pltpu.VMEM((count + 2 * TILE, ys), f32),
            pltpu.VMEM((2, own, LANES), f32),
            pltpu.VMEM((4, levels, LANES), f32),
        ),
        in_specs=[hbm] * 5,
        out_specs=(vmem,) * 3,
        scratch_shapes=[
            pltpu.VMEM(coefficients.shape, f32),
            pltpu.VMEM((1, spacing.shape[0]), f32),
            pltpu.VMEM(weights.shape, f32),
            pltpu.VMEM(basis.shape, jnp.bfloat16),
            pltpu.VMEM(twiddle.shape, f32),
            pltpu.VMEM((ys, 2 * modes), f32),
            pltpu.VMEM((2, groups, TILE, 2 * modes), f32),
            pltpu.VMEM((2 * width, 2 * modes), jnp.bfloat16),
            pltpu.VMEM((groups, own, LANES), f32),
            pltpu.VMEM((groups, block, LANES), f32),
            pltpu.VMEM((groups, own, LANES), f32),
            pltpu.VMEM((groups, block, LANES), f32),
            pltpu.VMEM((2, own, LANES), f32),
            pltpu.VMEM((TILE, LANES), f32),
            pltpu.VMEM((groups * columns, TILE, LANES), f32),
            pltpu.VMEM((groups, own, LANES), f32),
            dma((5,)),
            dma(()),
            dma((2,)),
            dma(()),
            dma((2,)),
            dma(()),
            dma((2,)),
            dma(()),
            dma(()),
            pltpu.SemaphoreType.REGULAR,
        ],
        compiler_params=pltpu.CompilerParams(
            collective_id=0, has_side_effects=True, vmem_limit_bytes=12 << 20
        ),
    )(*[
        pltpu.with_memory_space_constraint(jnp.asarray(x), pltpu.HBM)
        for x in (coefficients, spacing[None], weights, basis, twiddle)
    ])


def surface_by_gather(coefficients, spacing, groups):
    x_count = NX // groups
    x_first = lax.axis_index("gx") * x_count
    x_cells = x_first + jnp.arange(x_count, dtype=jnp.int32)
    portion = lax.all_gather(coefficients, "gx", axis=1, tiled=True)
    cosine, sine = basis(portion.shape[1], x_cells)
    surface = TOPO_SCALE * jnp.tanh(project(cosine, sine, portion) * 0.25)
    stretch = stretching(spacing)
    scale = stretch.shape[0] - 1.0
    slope = vertical(stretch)
    peak = lax.pmax(jnp.max(surface), ("gx", "gy"))
    wide = extended(surface, (("gx", 0), ("gy", 1)), 2)
    dx = (8.0 * (wide[3:-1] - wide[1:-3]) - (wide[4:] - wide[:-4]))[:, 2:-2] / 12.0
    dy = (8.0 * (wide[:, 3:-1] - wide[:, 1:-3]) - (wide[:, 4:] - wide[:, :-4]))[2:-2] / 12.0
    rows = [scale * stretch, scale * (1.0 - stretch), scale * slope]
    rows.append(slope / ((1.0 - peak) * jnp.min(slope)))
    table = jnp.broadcast_to(jnp.stack(rows)[:, :, None], (4, stretch.shape[0], LANES))
    return surface, dx, dy, table


def levels_kernel(depth, s_ref, dx_ref, dy_ref, table, z_ref, slopes_ref, jac_ref, quality_ref):
    first = pl.program_id(0) * depth

    def row(which, level):
        return table[which, pl.ds(first + level, 1), :]

    for level in range(depth):
        s, gain = s_ref[...], row(1, level)
        z_ref[level] = row(0, level) + gain * s
        slopes_ref[0, level] = gain * dx_ref[...]
        slopes_ref[1, level] = gain * dy_ref[...]
        rest = 1.0 - s
        jac_ref[level] = row(2, level) * rest
        quality_ref[level] = row(3, level) * rest


def all_levels(s, dx, dy, table):
    levels = table.shape[1]
    rows, columns = s.shape
    depth = 2
    plane = pl.BlockSpec((rows, columns), lambda i: (0, 0))
    field = pl.BlockSpec((depth, rows, columns), lambda i: (i, 0, 0))
    shape = jax.ShapeDtypeStruct((levels, rows, columns), jnp.float32)
    return pl.pallas_call(
        functools.partial(levels_kernel, depth),
        grid=(levels // depth,),
        in_specs=[plane, plane, plane, pl.BlockSpec(table.shape, lambda i: (0, 0, 0))],
        out_specs=(
            field,
            pl.BlockSpec((2, depth, rows, columns), lambda i: (0, i, 0, 0)),
            field,
            field,
        ),
        out_shape=(
            shape,
            jax.ShapeDtypeStruct((2, levels, rows, columns), jnp.float32),
            shape,
            shape,
        ),
    )(s, dx, dy, table)


def write_kernel(
    s_ref, sides, table, z_hbm, slopes_hbm, jac_hbm, quality_hbm,
    z, slopes, jac, quality, dx, dy, outer, sems,
):
    levels, count, _ = z.shape
    own = sides.shape[1]
    inner = pl.ds(TILE, count)

    def row(which, level):
        return table[which, pl.ds(level, 1), :]

    def heights(level, carry):
        s = s_ref[inner, :]
        z[level] = row(0, level) + row(1, level) * s
        pltpu.make_async_copy(z.at[level], z_hbm.at[level], sems.at[0]).start()
        rest = 1.0 - s
        jac[level] = row(2, level) * rest
        pltpu.make_async_copy(jac.at[level], jac_hbm.at[level], sems.at[2]).start()
        quality[level] = row(3, level) * rest
        pltpu.make_async_copy(quality.at[level], quality_hbm.at[level], sems.at[3]).start()
        return carry

    lax.fori_loop(0, levels, heights, 0)

    def near(by):
        return s_ref[pl.ds(TILE + by, count), :]

    dx[...] = (8.0 * (near(1) - near(-1)) - (near(2) - near(-2))) * (1.0 / 12.0)
    lane = lax.broadcasted_iota(jnp.int32, (own, LANES), 1)
    for r in range(RADIX):
        right, left = sides[0], sides[1]
        if r:
            right = pltpu.roll(right, LANES - r * TILE, 1)
        if r != RADIX - 1:
            left = pltpu.roll(left, LANES - TILE - r * TILE, 1)
        outer[pl.ds(r, own, stride=RADIX), :] = jnp.where(lane < LANES // 2, right, left)
    s, edge = s_ref[inner, :], outer[...]
    lane = lax.broadcasted_iota(jnp.int32, (count, LANES), 1)

    def moved(by):
        taken = lane < by if by > 0 else lane >= LANES + by
        return pltpu.roll(jnp.where(taken, edge, s), (LANES - by) % LANES, 1)

    dy[...] = (8.0 * (moved(1) - moved(-1)) - (moved(2) - moved(-2))) * (1.0 / 12.0)

    def tilts(level, carry):
        gain = row(1, level)
        for at, slope in enumerate((dx, dy)):
            slopes[at, level] = gain * slope[...]
            pltpu.make_async_copy(
                slopes.at[at, level], slopes_hbm.at[at, level], sems.at[1]
            ).start()
        return carry

    lax.fori_loop(0, levels, tilts, 0)
    for i, (src, dst) in enumerate(
        ((z, z_hbm), (slopes, slopes_hbm), (jac, jac_hbm), (quality, quality_hbm))
    ):
        pltpu.make_async_copy(src, dst, sems.at[i]).wait()


def write_all(s, sides, table):
    levels = table.shape[1]
    count, columns = s.shape[0] - 2 * TILE, s.shape[1]
    vmem = pl.BlockSpec(memory_space=pltpu.VMEM)
    hbm = pl.BlockSpec(memory_space=pl.ANY)
    field = (levels, count, columns)
    fields = (field, (2,) + field, field, field)
    f32 = jnp.float32
    plane = pltpu.VMEM((count, columns), f32)
    return pl.pallas_call(
        write_kernel,
        in_specs=[vmem] * 3,
        out_specs=(hbm,) * 4,
        out_shape=tuple(jax.ShapeDtypeStruct(shape, f32) for shape in fields),
        scratch_shapes=[pltpu.VMEM(shape, f32) for shape in fields]
        + [plane, plane, plane, pltpu.SemaphoreType.DMA((4,))],
        compiler_params=pltpu.CompilerParams(vmem_limit_bytes=48 << 20),
    )(s, sides, table)


def shards(coefficients, spacing):
    groups, columns = lax.axis_size("gx"), lax.axis_size("gy")
    _, modes, ys = coefficients.shape
    fits = (
        groups == 8
        and ys == LANES
        and ys == groups * RADIX
        and modes == NX // RADIX
        and modes % LANES == 0
        and columns > 1
    )
    if fits:
        return write_all(*surface_by_kernel(coefficients, spacing, groups, columns))
    return all_levels(*surface_by_gather(coefficients, spacing, groups))


def solution(mesh):
    return jax.shard_map(
        shards,
        mesh=mesh,
        in_specs=(P(None, "gx", "gy"), P()),
        out_specs=(
            P(None, "gx", "gy"),
            P(None, None, "gx", "gy"),
            P(None, "gx", "gy"),
            P(None, "gx", "gy"),
        ),
        check_vma=False,
    )
```

time: 38.4 us -> 30.9 us (0.80)
  Pallas kernels: 37.5 us -> 30.1 us
    pallas_call x1, Pallas kernels: 22.9 us -> 16.8 us  [surface_by_kernel(): pl.pallas_call(functools.partial(surface_kernel, groups, columns), out_sh...]
    pallas_call x1, Pallas kernels: 14.6 us -> 13.4 us  [write_all(): pl.pallas_call(write_kernel, in_specs=[vmem] * 3, out_specs=(hbm,) * 4, o...]
where the time goes in v1:
time: 30.9 us; the launch traced here: 30.8 us
  Pallas kernels  30.1 us (97%)
  between operations  0.64 us (2%)
    pallas_call x1, Pallas kernels, surface_by_kernel(): pl.pallas_call(functools.partial(surface_kernel, groups, columns), out_sh...  16.8 us
    pallas_call x1, Pallas kernels, write_all(): pl.pallas_call(write_kernel, in_specs=[vmem] * 3, out_specs=(hbm,) * 4, o...  13.4 us

profile of v1, /device:TPU:0, one launch (start us, length us, event | category | flops | bytes accessed | tf_op | source)
XLA Modules:
  0.0 30.8 jit_solution(15817863526409006294)
XLA Ops:
  0.6 16.8 %shard_map.84 = (f32[528,128]{1,0:T(8,128)S(1)}, f32[2,32,128]{2,1,0:T(8,128)S(1)}, f32[4,32,128]{2,1,0:T(8,128)S(1)}) custom-call(f32[2,256,128]{2,1,0:T(8,128)} %coef_hbm.1, f32[1,31]{1,0:T(1,128)} %bitcast.1, f32[2,32,31]{2,1,0:T(8,128)} %constant.6.clone.weights_hbm, bf16[640,512]{1,0:T(8,128)(2,1)} %constant.7.clone.basis_hbm, ...), custom_call_target="tpu_custom_call" | custom-call | tf_op jit(solution)/shard_map/pallas_call | solution.py:434
  17.4 13.4 %shard_map.85 = (f32[32,512,128]{2,1,0:T(8,128)}, f32[2,32,512,128]{3,2,1,0:T(8,128)}, f32[32,512,128]{2,1,0:T(8,128)}, f32[32,512,128]{2,1,0:T(8,128)}) custom-call(f32[528,128]{1,0:T(8,128)S(1)} %get-tuple-element.7.s_ref, f32[2,32,128]{2,1,0:T(8,128)S(1)} %get-tuple-element.8.sides, f32[4,32,128]{2,1,0:T(8,128)S(1)} %get-tuple-element.9.table), custom_call_target="tpu_custom_call" | custom-call | tf_op jit(solution)/shard_map/pallas_call | solution.py:612

commit v2 on v1

--- a/solution.py
+++ b/solution.py
@@ -104,19 +104,13 @@
     return np.stack([summed, deriv @ summed]).astype(np.float32)
 
 
-def transform_tables(modes, groups):
+def transform_tables():
     part = NX // RADIX
-    own = part // groups
-    block = own + TILE
-    rows = []
-    for dest in range(groups):
-        first = dest * own
-        rows += list(range(first, first + own)) + [first - 1, first + own] * (TILE // 2)
-    angle = 2.0 * np.pi / part * ((np.array(rows)[:, None] * np.arange(part)[None]) % part)
+    angle = 2.0 * np.pi / part * ((np.arange(part)[:, None] * np.arange(part)[None]) % part)
     full = np.concatenate([np.cos(angle), np.sin(angle)], axis=1).astype(np.float32)
     turn = 2.0 * np.pi / NX * (np.arange(RADIX)[:, None] * np.arange(part)[None])
     twiddle = np.concatenate([np.cos(turn), np.sin(turn)], axis=1).astype(np.float32)
-    return full, twiddle, block
+    return full, twiddle
 
 
 def rotate(value, angle):
@@ -170,17 +164,22 @@
     return [2 * j + (chunk + j // (groups // 2)) % 2 for j in range(groups)]
 
 
+def surface(raw):
+    return TOPO_SCALE * jnp.tanh(raw * 0.25)
+
+
 def arrived(view, sem):
     pltpu.make_async_copy(view, view, sem).wait()
 
 
 def surface_kernel(
     groups, columns, coef_hbm, spacing_hbm, weights_hbm, basis_hbm, twiddle_hbm,
-    s_out, sides, table,
+    s_out, sides, table, peak_out,
     coef, spacing, weights, basis, twiddle, turned, gathered, operand,
-    product_one, product_two, landed_one, landed_two, landed_sides, best, bests, partial,
-    load_sem, send_one, recv_one, send_two, recv_two, send_side, recv_side,
-    send_max, recv_max, later_sem,
+    product_one, product_two, landed_one, landed_two, ends, landed_ends,
+    side_parts, landed_sides, best, bests, partial,
+    load_sem, send_one, recv_one, send_two, recv_two, send_ends, recv_ends,
+    send_side, recv_side, send_max, recv_max, later_sem,
 ):
     gx, gy = lax.axis_index("gx"), lax.axis_index("gy")
     cores, rows_of = 2, groups // 2
@@ -202,9 +201,7 @@
             (basis_hbm, basis),
         ))
     ]
-    for load in loads:
-        load.start()
-
+    loads[0].start()
     barrier = pltpu.get_barrier_semaphore()
     for peer in peers:
         pl.semaphore_signal(barrier, inc=1, device_id=(peer, gy), device_id_type=MESH)
@@ -228,6 +225,8 @@
         return pl.ds(pl.multiple_of(target * ys + sub_of(chunk, target) * TILE, TILE), TILE)
 
     loads[0].wait()
+    for load in loads[1:]:
+        load.start()
     turned[:, :part] = coef[0].T
     turned[:, part:] = coef[1].T
     pl.semaphore_wait(barrier, groups - 1 + groups * gy)
@@ -265,10 +264,10 @@
     table[0] = jnp.broadcast_to(scale * stretch, (levels, LANES))
     table[1] = jnp.broadcast_to(scale * (1.0 - stretch), (levels, LANES))
     table[2] = jnp.broadcast_to(scale * slope, (levels, LANES))
+    table[3] = jnp.broadcast_to(slope / least, (levels, LANES))
 
     rows = basis.shape[0] // 2
-    block = rows // groups
-    own = block - TILE
+    own = rows // groups
     count = own * RADIX
     width = RADIX * TILE
     dot = functools.partial(
@@ -312,59 +311,110 @@
     def tallest(raw):
         return functools.reduce(jnp.maximum, [raw[i : i + TILE] for i in range(0, rows, TILE)])
 
+    row_lane = lax.broadcasted_iota(jnp.int32, (1, LANES), 1)
+
+    def ends_of(raw):
+        return [
+            jnp.where(
+                row_lane < LANES // 2,
+                raw[(dest + 1) * own % rows : (dest + 1) * own % rows + 1],
+                raw[(dest * own - 1) % rows : (dest * own - 1) % rows + 1],
+            )
+            for dest in range(groups)
+        ]
+
+    def send_best(target, slot):
+        for d in range(groups):
+            pltpu.make_async_remote_copy(
+                src_ref=best,
+                dst_ref=bests.at[slot * groups + gx],
+                send_sem=send_max,
+                recv_sem=recv_max,
+                device_id=(lax.rem(gx + d, groups), target),
+                device_id_type=MESH,
+            ).start()
+
+    lane_one = lax.broadcasted_iota(jnp.int32, (TILE, LANES), 1)
+
+    def pack_sides(which):
+        for dest in range(groups):
+            packed = None
+            for k in range(own // TILE):
+                shift = (2 * k - which * (TILE - 2)) % LANES
+                tile = product_one[dest, k * TILE : (k + 1) * TILE]
+                tile = pltpu.roll(tile, shift, 1) if shift else tile
+                packed = tile if k == 0 else jnp.where(lane_one % TILE // 2 == k, tile, packed)
+            side_parts[dest] = packed
+
+    def send_sides(to_lower):
+        for which, sender in enumerate((0, groups - 1)):
+            column = lax.rem(gy + (columns - 1, 1)[which], columns)
+
+            @pl.when(jnp.logical_and(gx == sender, (column < gy) if to_lower else (column > gy)))
+            def _():
+                for dest in range(groups):
+                    pltpu.make_async_remote_copy(
+                        src_ref=side_parts.at[dest],
+                        dst_ref=landed_sides.at[which],
+                        send_sem=send_side,
+                        recv_sem=recv_side.at[which],
+                        device_id=(dest, column),
+                        device_id_type=MESH,
+                    ).start()
+
     arrived(gathered.at[0, pl.ds(0, groups - 1)], recv_one.at[0])
     raw = transform(0)
-    ends_one = [raw[dest * block + own : (dest + 1) * block] for dest in range(groups)]
     for dest in range(groups):
-        product_one[dest] = raw[dest * block : dest * block + own]
+        product_one[dest] = raw[dest * own : (dest + 1) * own]
     send_product(product_one, landed_one, 0)
+    ends_one = ends_of(raw)
     peak_one = tallest(raw)
+
+    for which, sender in enumerate((0, groups - 1)):
+        pl.when(gx == sender)(functools.partial(pack_sides, which))
+    send_sides(True)
+
+    arrived(gathered.at[1, pl.ds(0, groups - 1)], recv_one.at[1])
+    raw = transform(1)
+    for dest in range(groups):
+        product_two[dest] = raw[dest * own : (dest + 1) * own]
+    best[...] = jnp.max(jnp.maximum(peak_one, tallest(raw)), axis=0, keepdims=True)
+    for down in range(columns - 1, 0, -1):
+
+        @pl.when(gy >= down)
+        def _():
+            send_best(gy - down, down - 1)
+
+    send_product(product_two, landed_two, 1)
+    ends_two = ends_of(raw)
+    outside = jnp.abs(row_lane // TILE * 2 - (RADIX - 1)) > RADIX // 2
+    for dest in range(groups):
+        one, two = ends_one[dest], ends_two[dest]
+        low, high = jnp.where(flip == 0, one, two), jnp.where(flip == 0, two, one)
+        ends[dest, 0:1] = jnp.where(outside, low, pltpu.roll(high, LANES // 2, 1))
+        ends[dest, 1:2] = best[...]
+    for target in peers:
+        pltpu.make_async_remote_copy(
+            src_ref=ends.at[target],
+            dst_ref=landed_ends.at[gx],
+            send_sem=send_ends,
+            recv_sem=recv_ends,
+            device_id=(target, gy),
+            device_id_type=MESH,
+        ).start()
+    landed_ends[gx] = ends[gx]
 
     @pl.when(gy < columns - 1)
     def _():
         pl.semaphore_wait(later_sem, groups * (columns - 1 - gy))
 
-    for which, sender in enumerate((0, groups - 1)):
-
-        @pl.when(gx == sender)
+    send_sides(False)
+
+    for up in range(1, columns):
+
+        @pl.when(gy + up < columns)
         def _():
-            for dest in range(groups):
-                pltpu.make_async_remote_copy(
-                    src_ref=product_one.at[dest],
-                    dst_ref=landed_sides.at[which],
-                    send_sem=send_side,
-                    recv_sem=recv_side.at[which],
-                    device_id=(dest, lax.rem(gy + (columns - 1, 1)[which], columns)),
-                    device_id_type=MESH,
-                ).start()
-
-    arrived(gathered.at[1, pl.ds(0, groups - 1)], recv_one.at[1])
-    raw = transform(1)
-    sublane = lax.broadcasted_iota(jnp.int32, (TILE, LANES), 0)
-    for dest in range(groups):
-        product_two[dest, :own] = raw[dest * block : dest * block + own]
-        product_two[dest, own:] = jnp.where(
-            sublane < 2, ends_one[dest], raw[dest * block + own : (dest + 1) * block]
-        )
-    send_product(product_two, landed_two, 1)
-    best[...] = jnp.broadcast_to(
-        jnp.max(jnp.maximum(peak_one, tallest(raw)), keepdims=True), (TILE, LANES)
-    )
-    for d in range(1, groups * columns):
-        pltpu.make_async_remote_copy(
-            src_ref=best,
-            dst_ref=bests.at[d],
-            send_sem=send_max,
-            recv_sem=recv_max,
-            device_id=(
-                lax.rem(gx + d // columns, groups),
-                lax.rem(gy + d % columns, columns),
-            ),
-            device_id_type=MESH,
-        ).start()
-
-    def surface(piece):
-        return TOPO_SCALE * jnp.tanh(piece * 0.25)
+            send_best(gy + up, columns - up - 1)
 
     lane = lax.broadcasted_iota(jnp.int32, (own, LANES), 1)
     arrived(landed_one.at[pl.ds(0, groups - 1)], recv_two.at[0])
@@ -375,7 +425,7 @@
         partial[b // 2] = value
 
     arrived(landed_two.at[pl.ds(0, groups - 1)], recv_two.at[1])
-    second = {b: surface(landed_two[j, :own]) for j, b in enumerate(blocks_of(1, groups))}
+    second = {b: surface(landed_two[j]) for j, b in enumerate(blocks_of(1, groups))}
     for bit in (2, 4):
         second = butterfly(second, bit, lane)
     pieces = {b: partial[b // 2] for b in first} | second
@@ -384,17 +434,18 @@
     for r in range(RADIX):
         s_out[pl.ds(TILE + r, own, stride=RADIX), :] = pieces[r]
 
-    lane = lax.broadcasted_iota(jnp.int32, (TILE, LANES), 1)
-    ends = {b: surface(landed_two[b // 2, own:]) for b in range(2 * groups)}
-    for bit in (2, 4, 8, 1):
-        ends = butterfly(ends, bit, lane)
-    is_late = lax.rem(lane // TILE + lane // (LANES // 2), 2)[0:1] == 1
-    for i in range(2):
-        before, after = ends[RADIX - 2 + i], ends[i]
-        s_out[TILE - 2 + i : TILE - 1 + i, :] = jnp.where(is_late, before[2:3], before[0:1])
-        s_out[TILE + count + i : TILE + count + i + 1, :] = jnp.where(
-            is_late, after[3:4], after[1:2]
-        )
+    arrived(landed_ends.at[pl.ds(0, groups - 1)], recv_ends)
+    edge = pltpu.roll(surface(landed_ends[:, 0, :]), 0, 1, stride=2 * TILE, stride_axis=0)
+    lane = lax.broadcasted_iota(jnp.int32, (groups, LANES), 1)
+    source = lax.broadcasted_iota(jnp.int32, (groups, LANES), 0)
+    for at, r in ((-2, RADIX - 2), (-1, RADIX - 1), (count, 0), (count + 1, 1)):
+        total_row = None
+        for sub in range(2):
+            shift = (sub - (r - sub * RADIX // 2)) * TILE % LANES
+            moved = pltpu.roll(edge, shift, 1) if shift else edge
+            moved = jnp.where(lane // TILE == 2 * source + sub, moved, 0.0)
+            total_row = moved if sub == 0 else total_row + moved
+        s_out[TILE + at : TILE + at + 1, :] = jnp.sum(total_row, axis=0, keepdims=True)
 
     for which in range(2):
         arrived(landed_sides.at[which], recv_side.at[which])
@@ -403,29 +454,30 @@
     arrived(turned.at[pl.ds(0, (groups - 1) * ys)], send_one)
     arrived(product_one.at[pl.ds(0, groups - 1)], send_two)
     arrived(product_two.at[pl.ds(0, groups - 1)], send_two)
+    arrived(ends.at[pl.ds(0, groups - 1)], send_ends)
 
     @pl.when(jnp.logical_or(gx == 0, gx == groups - 1))
     def _():
-        arrived(product_one, send_side)
-
-    arrived(bests.at[pl.ds(1, groups * columns - 1)], recv_max)
-    arrived(bests.at[pl.ds(1, groups * columns - 1)], send_max)
-    peak = best[0:1, :]
-    for d in range(1, groups * columns):
-        peak = jnp.maximum(peak, bests[d, 0:1, :])
-    table[3] = jnp.broadcast_to(slope, (levels, LANES)) / ((1.0 - surface(peak)) * least)
+        arrived(side_parts, send_side)
+
+    arrived(bests, recv_max)
+    arrived(bests, send_max)
+    peak = jnp.max(landed_ends[:, 1, :], axis=0, keepdims=True)
+    for d in range(groups * (columns - 1)):
+        peak = jnp.maximum(peak, bests[d])
+    peak_out[...] = peak
 
 
 def surface_by_kernel(coefficients, spacing, groups, columns):
     _, modes, ys = coefficients.shape
-    full, twiddle, block = transform_tables(modes * groups, groups)
+    full, twiddle = transform_tables()
     high = full.astype(jnp.bfloat16)
     low = (full - high.astype(np.float32)).astype(jnp.bfloat16)
     basis = np.concatenate([high, low], axis=0)
     weights = level_weights(spacing.shape[0])
     levels = spacing.shape[0] + 1
     count = NX // groups
-    own = block - TILE
+    own = count // RADIX
     width = RADIX * TILE
     vmem = pl.BlockSpec(memory_space=pltpu.VMEM)
     hbm = pl.BlockSpec(memory_space=pltpu.HBM)
@@ -435,11 +487,12 @@
         functools.partial(surface_kernel, groups, columns),
         out_shape=(
             pltpu.VMEM((count + 2 * TILE, ys), f32),
-            pltpu.VMEM((2, own, LANES), f32),
+            pltpu.VMEM((2, TILE, LANES), f32),
             pltpu.VMEM((4, levels, LANES), f32),
+            pltpu.VMEM((1, LANES), f32),
         ),
         in_specs=[hbm] * 5,
-        out_specs=(vmem,) * 3,
+        out_specs=(vmem,) * 4,
         scratch_shapes=[
             pltpu.VMEM(coefficients.shape, f32),
             pltpu.VMEM((1, spacing.shape[0]), f32),
@@ -449,19 +502,23 @@
             pltpu.VMEM((ys, 2 * modes), f32),
             pltpu.VMEM((2, groups, TILE, 2 * modes), f32),
             pltpu.VMEM((2 * width, 2 * modes), jnp.bfloat16),
-            pltpu.VMEM((groups, own, LANES), f32),
-            pltpu.VMEM((groups, block, LANES), f32),
-            pltpu.VMEM((groups, own, LANES), f32),
-            pltpu.VMEM((groups, block, LANES), f32),
-            pltpu.VMEM((2, own, LANES), f32),
-            pltpu.VMEM((TILE, LANES), f32),
-            pltpu.VMEM((groups * columns, TILE, LANES), f32),
+        ]
+        + [pltpu.VMEM((groups, own, LANES), f32)] * 4
+        + [
+            pltpu.VMEM((groups, 2, LANES), f32),
+            pltpu.VMEM((groups, 2, LANES), f32),
+            pltpu.VMEM((groups, TILE, LANES), f32),
+            pltpu.VMEM((2, TILE, LANES), f32),
+            pltpu.VMEM((1, LANES), f32),
+            pltpu.VMEM((groups * (columns - 1), 1, LANES), f32),
             pltpu.VMEM((groups, own, LANES), f32),
             dma((5,)),
             dma(()),
             dma((2,)),
             dma(()),
             dma((2,)),
+            dma(()),
+            dma(()),
             dma(()),
             dma((2,)),
             dma(()),
@@ -540,41 +597,44 @@
 
 
 def write_kernel(
-    s_ref, sides, table, z_hbm, slopes_hbm, jac_hbm, quality_hbm,
-    z, slopes, jac, quality, dx, dy, outer, sems,
+    s_ref, sides, table, peak, z_hbm, slopes_hbm, jac_hbm, quality_hbm,
+    z, slopes, jac, quality, dx, dy, outer, scaled, sems,
 ):
     levels, count, _ = z.shape
-    own = sides.shape[1]
+    own = count // RADIX
     inner = pl.ds(TILE, count)
 
     def row(which, level):
         return table[which, pl.ds(level, 1), :]
+
+    def put(src, dst, at, which):
+        pltpu.make_async_copy(src.at[at], dst.at[at], sems.at[which]).start()
 
     def heights(level, carry):
         s = s_ref[inner, :]
         z[level] = row(0, level) + row(1, level) * s
-        pltpu.make_async_copy(z.at[level], z_hbm.at[level], sems.at[0]).start()
-        rest = 1.0 - s
-        jac[level] = row(2, level) * rest
-        pltpu.make_async_copy(jac.at[level], jac_hbm.at[level], sems.at[2]).start()
-        quality[level] = row(3, level) * rest
-        pltpu.make_async_copy(quality.at[level], quality_hbm.at[level], sems.at[3]).start()
+        put(z, z_hbm, level, 0)
+        jac[level] = row(2, level) * (1.0 - s)
+        put(jac, jac_hbm, level, 2)
         return carry
 
     lax.fori_loop(0, levels, heights, 0)
+    highest = surface(jnp.max(peak[...], axis=1, keepdims=True))
+    scaled[...] = table[3] / (1.0 - highest)
 
     def near(by):
         return s_ref[pl.ds(TILE + by, count), :]
 
     dx[...] = (8.0 * (near(1) - near(-1)) - (near(2) - near(-2))) * (1.0 / 12.0)
-    lane = lax.broadcasted_iota(jnp.int32, (own, LANES), 1)
+    lane = lax.broadcasted_iota(jnp.int32, (TILE, LANES), 1)
     for r in range(RADIX):
-        right, left = sides[0], sides[1]
-        if r:
-            right = pltpu.roll(right, LANES - r * TILE, 1)
-        if r != RADIX - 1:
-            left = pltpu.roll(left, LANES - TILE - r * TILE, 1)
-        outer[pl.ds(r, own, stride=RADIX), :] = jnp.where(lane < LANES // 2, right, left)
+        for k in range(own // TILE):
+            shift = LANES - r * TILE - 2 * k
+            right = pltpu.roll(sides[0], shift % LANES, 1) if shift % LANES else sides[0]
+            left = pltpu.roll(sides[1], (shift - 2) % LANES, 1) if (shift - 2) % LANES else sides[1]
+            outer[pl.ds(k * TILE * RADIX + r, TILE, stride=RADIX), :] = jnp.where(
+                lane < LANES // 2, right, left
+            )
     s, edge = s_ref[inner, :], outer[...]
     lane = lax.broadcasted_iota(jnp.int32, (count, LANES), 1)
 
@@ -588,9 +648,9 @@
         gain = row(1, level)
         for at, slope in enumerate((dx, dy)):
             slopes[at, level] = gain * slope[...]
-            pltpu.make_async_copy(
-                slopes.at[at, level], slopes_hbm.at[at, level], sems.at[1]
-            ).start()
+            put(slopes, slopes_hbm, (at, level), 1)
+        quality[level] = scaled[pl.ds(level, 1), :] * (1.0 - s_ref[inner, :])
+        put(quality, quality_hbm, level, 3)
         return carry
 
     lax.fori_loop(0, levels, tilts, 0)
@@ -600,7 +660,7 @@
         pltpu.make_async_copy(src, dst, sems.at[i]).wait()
 
 
-def write_all(s, sides, table):
+def write_all(s, sides, table, peak):
     levels = table.shape[1]
     count, columns = s.shape[0] - 2 * TILE, s.shape[1]
     vmem = pl.BlockSpec(memory_space=pltpu.VMEM)
@@ -611,13 +671,13 @@
     plane = pltpu.VMEM((count, columns), f32)
     return pl.pallas_call(
         write_kernel,
-        in_specs=[vmem] * 3,
+        in_specs=[vmem] * 4,
         out_specs=(hbm,) * 4,
         out_shape=tuple(jax.ShapeDtypeStruct(shape, f32) for shape in fields),
         scratch_shapes=[pltpu.VMEM(shape, f32) for shape in fields]
-        + [plane, plane, plane, pltpu.SemaphoreType.DMA((4,))],
+        + [plane, plane, plane, pltpu.VMEM((levels, LANES), f32), pltpu.SemaphoreType.DMA((4,))],
         compiler_params=pltpu.CompilerParams(vmem_limit_bytes=48 << 20),
-    )(s, sides, table)
+    )(s, sides, table, peak)
 
 
 def shards(coefficients, spacing):

time: 30.9 us -> 29.5 us (0.955)
  Pallas kernels: 30.1 us -> 28.7 us
    pallas_call x1, Pallas kernels: 16.8 us -> 15.3 us  [surface_by_kernel(): pl.pallas_call(functools.partial(surface_kernel, groups, columns), out_sh...]
where the time goes in v2:
time: 29.5 us; the launch traced here: 29.3 us
  Pallas kernels  28.7 us (97%)
  between operations  0.64 us (2%)
    pallas_call x1, Pallas kernels, surface_by_kernel(): pl.pallas_call(functools.partial(surface_kernel, groups, columns), out_sh...  15.3 us
    pallas_call x1, Pallas kernels, write_all(): pl.pallas_call(write_kernel, in_specs=[vmem] * 4, out_specs=(hbm,) * 4, o...  13.4 us

profile of v2, /device:TPU:0, one launch (start us, length us, event | category | flops | bytes accessed | tf_op | source)
XLA Modules:
  0.0 29.3 jit_solution(18421438380792178272)
XLA Ops:
  0.6 15.3 %shard_map.84 = (f32[528,128]{1,0:T(8,128)S(1)}, f32[2,8,128]{2,1,0:T(8,128)S(1)}, f32[4,32,128]{2,1,0:T(8,128)S(1)}, f32[1,128]{1,0:T(1,128)S(1)}) custom-call(f32[2,256,128]{2,1,0:T(8,128)} %coef_hbm.1, f32[1,31]{1,0:T(1,128)} %bitcast.1, f32[2,32,31]{2,1,0:T(8,128)} %constant.6.clone.weights_hbm, bf16[512,512]{1,0:T(8,128)(2,1)} %constant.7.clone.basis_hbm, ...), custom_call_target="tpu_custom_call" | custom-call | tf_op jit(solution)/shard_map/pallas_call | solution.py:486
  16.0 13.4 %shard_map.85 = (f32[32,512,128]{2,1,0:T(8,128)}, f32[2,32,512,128]{3,2,1,0:T(8,128)}, f32[32,512,128]{2,1,0:T(8,128)}, f32[32,512,128]{2,1,0:T(8,128)}) custom-call(f32[528,128]{1,0:T(8,128)S(1)} %get-tuple-element.8.s_ref, f32[2,8,128]{2,1,0:T(8,128)S(1)} %get-tuple-element.9.sides, f32[4,32,128]{2,1,0:T(8,128)S(1)} %get-tuple-element.10.table, ...), custom_call_target="tpu_custom_call" | custom-call | tf_op jit(solution)/shard_map/pallas_call | solution.py:672

commit v3 on v2

--- a/solution.py
+++ b/solution.py
@@ -231,16 +231,17 @@
     turned[:, part:] = coef[1].T
     pl.semaphore_wait(barrier, groups - 1 + groups * gy)
 
-    for chunk in range(2):
-        for target in peers:
-            pltpu.make_async_remote_copy(
-                src_ref=turned.at[turned_rows(chunk, target)],
-                dst_ref=gathered.at[chunk, gx],
-                send_sem=send_one,
-                recv_sem=recv_one.at[chunk],
-                device_id=(target, gy),
-                device_id_type=MESH,
-            ).start()
+    far, close = peers[:2], peers[2:]
+    order = [(chunk, peer) for some in (far, close) for chunk in range(2) for peer in some]
+    for chunk, target in order:
+        pltpu.make_async_remote_copy(
+            src_ref=turned.at[turned_rows(chunk, target)],
+            dst_ref=gathered.at[chunk, gx],
+            send_sem=send_one,
+            recv_sem=recv_one.at[chunk],
+            device_id=(target, gy),
+            device_id_type=MESH,
+        ).start()
     for down in range(1, columns):
 
         @pl.when(gy >= down)
@@ -336,13 +337,12 @@
 
     lane_one = lax.broadcasted_iota(jnp.int32, (TILE, LANES), 1)
 
-    def pack_sides(which):
+    def pack_sides():
         for dest in range(groups):
             packed = None
             for k in range(own // TILE):
-                shift = (2 * k - which * (TILE - 2)) % LANES
-                tile = product_one[dest, k * TILE : (k + 1) * TILE]
-                tile = pltpu.roll(tile, shift, 1) if shift else tile
+                shift = jnp.where(flip == 0, 2 * k, (2 * k + 2 - TILE) % LANES)
+                tile = pltpu.roll(product_one[dest, k * TILE : (k + 1) * TILE], shift, 1)
                 packed = tile if k == 0 else jnp.where(lane_one % TILE // 2 == k, tile, packed)
             side_parts[dest] = packed
 
@@ -370,20 +370,20 @@
     ends_one = ends_of(raw)
     peak_one = tallest(raw)
 
-    for which, sender in enumerate((0, groups - 1)):
-        pl.when(gx == sender)(functools.partial(pack_sides, which))
-    send_sides(True)
-
     arrived(gathered.at[1, pl.ds(0, groups - 1)], recv_one.at[1])
     raw = transform(1)
     for dest in range(groups):
         product_two[dest] = raw[dest * own : (dest + 1) * own]
+    pack_sides()
     best[...] = jnp.max(jnp.maximum(peak_one, tallest(raw)), axis=0, keepdims=True)
     for down in range(columns - 1, 0, -1):
 
         @pl.when(gy >= down)
         def _():
             send_best(gy - down, down - 1)
+
+        if down == columns - 1:
+            send_sides(True)
 
     send_product(product_two, landed_two, 1)
     ends_two = ends_of(raw)

time: 29.5 us -> 29 us (0.983)
  Pallas kernels: 28.7 us -> 28.2 us
    pallas_call x1, Pallas kernels: 15.3 us -> 14.9 us  [surface_by_kernel(): pl.pallas_call(functools.partial(surface_kernel, groups, columns), out_sh...]
where the time goes in v3:
time: 29 us; the launch traced here: 28.9 us
  Pallas kernels  28.2 us (97%)
  between operations  0.64 us (2%)
    pallas_call x1, Pallas kernels, surface_by_kernel(): pl.pallas_call(functools.partial(surface_kernel, groups, columns), out_sh...  14.9 us
    pallas_call x1, Pallas kernels, write_all(): pl.pallas_call(write_kernel, in_specs=[vmem] * 4, out_specs=(hbm,) * 4, o...  13.4 us

profile of v3, /device:TPU:0, one launch (start us, length us, event | category | flops | bytes accessed | tf_op | source)
XLA Modules:
  0.0 28.9 jit_solution(12959533215438698654)
XLA Ops:
  0.6 14.9 %shard_map.84 = (f32[528,128]{1,0:T(8,128)S(1)}, f32[2,8,128]{2,1,0:T(8,128)S(1)}, f32[4,32,128]{2,1,0:T(8,128)S(1)}, f32[1,128]{1,0:T(1,128)S(1)}) custom-call(f32[2,256,128]{2,1,0:T(8,128)} %coef_hbm.1, f32[1,31]{1,0:T(1,128)} %bitcast.1, f32[2,32,31]{2,1,0:T(8,128)} %constant.6.clone.weights_hbm, bf16[512,512]{1,0:T(8,128)(2,1)} %constant.7.clone.basis_hbm, ...), custom_call_target="tpu_custom_call" | custom-call | tf_op jit(solution)/shard_map/pallas_call | solution.py:486
  15.5 13.4 %shard_map.85 = (f32[32,512,128]{2,1,0:T(8,128)}, f32[2,32,512,128]{3,2,1,0:T(8,128)}, f32[32,512,128]{2,1,0:T(8,128)}, f32[32,512,128]{2,1,0:T(8,128)}) custom-call(f32[528,128]{1,0:T(8,128)S(1)} %get-tuple-element.8.s_ref, f32[2,8,128]{2,1,0:T(8,128)S(1)} %get-tuple-element.9.sides, f32[4,32,128]{2,1,0:T(8,128)S(1)} %get-tuple-element.10.table, ...), custom_call_target="tpu_custom_call" | custom-call | tf_op jit(solution)/shard_map/pallas_call | solution.py:672

commit v4 on v3

--- a/solution.py
+++ b/solution.py
@@ -297,8 +297,9 @@
         both = dot(basis[:rows], operand[...])
         return both[:, :width] + both[:, width:] + dot(basis[rows:], operand[:width])
 
-    def send_product(product, landed, chunk):
-        for target in peers:
+    def send_product(chunk, some):
+        product, landed = ((product_one, landed_one), (product_two, landed_two))[chunk]
+        for target in some:
             pltpu.make_async_remote_copy(
                 src_ref=product.at[target],
                 dst_ref=landed.at[gx],
@@ -307,7 +308,6 @@
                 device_id=(target, gy),
                 device_id_type=MESH,
             ).start()
-        landed[gx] = product[gx]
 
     def tallest(raw):
         return functools.reduce(jnp.maximum, [raw[i : i + TILE] for i in range(0, rows, TILE)])
@@ -366,7 +366,11 @@
     raw = transform(0)
     for dest in range(groups):
         product_one[dest] = raw[dest * own : (dest + 1) * own]
-    send_product(product_one, landed_one, 0)
+    @pl.when(gy < columns - 1)
+    def _():
+        send_product(0, far + close[2:])
+
+    landed_one[gx] = product_one[gx]
     ends_one = ends_of(raw)
     peak_one = tallest(raw)
 
@@ -385,7 +389,19 @@
         if down == columns - 1:
             send_sides(True)
 
-    send_product(product_two, landed_two, 1)
+    @pl.when(gy == columns - 1)
+    def _():
+        send_product(0, far)
+        send_product(1, far)
+        send_product(0, close)
+
+    @pl.when(gy < columns - 1)
+    def _():
+        send_product(1, far)
+        send_product(0, close[:2])
+
+    send_product(1, close[2:] + close[:2])
+    landed_two[gx] = product_two[gx]
     ends_two = ends_of(raw)
     outside = jnp.abs(row_lane // TILE * 2 - (RADIX - 1)) > RADIX // 2
     for dest in range(groups):

time: 29 us -> 29 us (level)
  no operation moved by 1% of the time
where the time goes in v4:
time: 29 us; the launch traced here: 28.9 us
  Pallas kernels  28.2 us (97%)
  between operations  0.64 us (2%)
    pallas_call x1, Pallas kernels, surface_by_kernel(): pl.pallas_call(functools.partial(surface_kernel, groups, columns), out_sh...  14.9 us
    pallas_call x1, Pallas kernels, write_all(): pl.pallas_call(write_kernel, in_specs=[vmem] * 4, out_specs=(hbm,) * 4, o...  13.4 us

profile of v4, /device:TPU:0, one launch (start us, length us, event | category | flops | bytes accessed | tf_op | source)
XLA Modules:
  0.0 28.9 jit_solution(6906618017212926286)
XLA Ops:
  0.6 14.9 %shard_map.84 = (f32[528,128]{1,0:T(8,128)S(1)}, f32[2,8,128]{2,1,0:T(8,128)S(1)}, f32[4,32,128]{2,1,0:T(8,128)S(1)}, f32[1,128]{1,0:T(1,128)S(1)}) custom-call(f32[2,256,128]{2,1,0:T(8,128)} %coef_hbm.1, f32[1,31]{1,0:T(1,128)} %bitcast.1, f32[2,32,31]{2,1,0:T(8,128)} %constant.6.clone.weights_hbm, bf16[512,512]{1,0:T(8,128)(2,1)} %constant.7.clone.basis_hbm, ...), custom_call_target="tpu_custom_call" | custom-call | tf_op jit(solution)/shard_map/pallas_call | solution.py:502
  15.5 13.4 %shard_map.85 = (f32[32,512,128]{2,1,0:T(8,128)}, f32[2,32,512,128]{3,2,1,0:T(8,128)}, f32[32,512,128]{2,1,0:T(8,128)}, f32[32,512,128]{2,1,0:T(8,128)}) custom-call(f32[528,128]{1,0:T(8,128)S(1)} %get-tuple-element.8.s_ref, f32[2,8,128]{2,1,0:T(8,128)S(1)} %get-tuple-element.9.sides, f32[4,32,128]{2,1,0:T(8,128)S(1)} %get-tuple-element.10.table, ...), custom_call_target="tpu_custom_call" | custom-call | tf_op jit(solution)/shard_map/pallas_call | solution.py:688

commit v5 on v3

--- a/solution.py
+++ b/solution.py
@@ -183,12 +183,13 @@
 ):
     gx, gy = lax.axis_index("gx"), lax.axis_index("gy")
     cores, rows_of = 2, groups // 2
+    flip = gx // rows_of
+    col, core = gx // cores - flip * (rows_of // cores), gx - gx // cores * cores
 
     def other(d):
-        core = lax.rem(gx + d % cores, cores)
-        row = lax.rem(gx // rows_of + d // rows_of, 2)
-        col = lax.rem(gx // cores + (d // cores) % 2, 2)
-        return row * rows_of + col * cores + core
+        places = (flip, d // rows_of), (col, d // cores % 2), (core, d % cores)
+        row_to, col_to, core_to = [1 - at if moves else at for at, moves in places]
+        return row_to * rows_of + col_to * cores + core_to
 
     peers = [other(d) for d in (6, 7, 2, 3, 4, 5, 1)]
     loads = [
@@ -216,7 +217,6 @@
     part = coef.shape[1]
     ys = coef.shape[2] // groups
     half = NX // RADIX
-    flip = gx // rows_of
 
     def sub_of(chunk, target):
         return lax.rem(chunk + target // rows_of, 2)
@@ -294,8 +294,9 @@
                 high, low = split(jnp.concatenate([pair[0][at], pair[1][at]], axis=0))
                 operand[r * TILE : (r + 2) * TILE, lanes] = high
                 operand[width + r * TILE : width + (r + 2) * TILE, lanes] = low
+        small = dot(basis[rows:], operand[:width])
         both = dot(basis[:rows], operand[...])
-        return both[:, :width] + both[:, width:] + dot(basis[rows:], operand[:width])
+        return both[:, :width] + (both[:, width:] + small)
 
     def send_product(product, landed, chunk):
         for target in peers:
@@ -374,7 +375,6 @@
     raw = transform(1)
     for dest in range(groups):
         product_two[dest] = raw[dest * own : (dest + 1) * own]
-    pack_sides()
     best[...] = jnp.max(jnp.maximum(peak_one, tallest(raw)), axis=0, keepdims=True)
     for down in range(columns - 1, 0, -1):
 
@@ -383,6 +383,7 @@
             send_best(gy - down, down - 1)
 
         if down == columns - 1:
+            pack_sides()
             send_sides(True)
 
     send_product(product_two, landed_two, 1)

time: 29 us -> 29 us (level)
  no operation moved by 1% of the time
where the time goes in v5:
time: 29 us; the launch traced here: 28.8 us
  Pallas kernels  28.2 us (97%)
  between operations  0.64 us (2%)
    pallas_call x1, Pallas kernels, surface_by_kernel(): pl.pallas_call(functools.partial(surface_kernel, groups, columns), out_sh...  14.8 us
    pallas_call x1, Pallas kernels, write_all(): pl.pallas_call(write_kernel, in_specs=[vmem] * 4, out_specs=(hbm,) * 4, o...  13.4 us

profile of v5, /device:TPU:0, one launch (start us, length us, event | category | flops | bytes accessed | tf_op | source)
XLA Modules:
  0.0 28.8 jit_solution(7394204463766805882)
XLA Ops:
  0.6 14.8 %shard_map.84 = (f32[528,128]{1,0:T(8,128)S(1)}, f32[2,8,128]{2,1,0:T(8,128)S(1)}, f32[4,32,128]{2,1,0:T(8,128)S(1)}, f32[1,128]{1,0:T(1,128)S(1)}) custom-call(f32[2,256,128]{2,1,0:T(8,128)} %coef_hbm.1, f32[1,31]{1,0:T(1,128)} %bitcast.1, f32[2,32,31]{2,1,0:T(8,128)} %constant.6.clone.weights_hbm, bf16[512,512]{1,0:T(8,128)(2,1)} %constant.7.clone.basis_hbm, ...), custom_call_target="tpu_custom_call" | custom-call | tf_op jit(solution)/shard_map/pallas_call | solution.py:487
  15.5 13.4 %shard_map.85 = (f32[32,512,128]{2,1,0:T(8,128)}, f32[2,32,512,128]{3,2,1,0:T(8,128)}, f32[32,512,128]{2,1,0:T(8,128)}, f32[32,512,128]{2,1,0:T(8,128)}) custom-call(f32[528,128]{1,0:T(8,128)S(1)} %get-tuple-element.8.s_ref, f32[2,8,128]{2,1,0:T(8,128)S(1)} %get-tuple-element.9.sides, f32[4,32,128]{2,1,0:T(8,128)S(1)} %get-tuple-element.10.table, ...), custom_call_target="tpu_custom_call" | custom-call | tf_op jit(solution)/shard_map/pallas_call | solution.py:673

commit v6 on v5

--- a/solution.py
+++ b/solution.py
@@ -298,8 +298,9 @@
         both = dot(basis[:rows], operand[...])
         return both[:, :width] + (both[:, width:] + small)
 
-    def send_product(product, landed, chunk):
-        for target in peers:
+    def send_product(chunk, some):
+        product, landed = ((product_one, landed_one), (product_two, landed_two))[chunk]
+        for target in some:
             pltpu.make_async_remote_copy(
                 src_ref=product.at[target],
                 dst_ref=landed.at[gx],
@@ -308,7 +309,6 @@
                 device_id=(target, gy),
                 device_id_type=MESH,
             ).start()
-        landed[gx] = product[gx]
 
     def tallest(raw):
         return functools.reduce(jnp.maximum, [raw[i : i + TILE] for i in range(0, rows, TILE)])
@@ -367,7 +367,9 @@
     raw = transform(0)
     for dest in range(groups):
         product_one[dest] = raw[dest * own : (dest + 1) * own]
-    send_product(product_one, landed_one, 0)
+    by_col, by_row, twin = close[:2], close[2:4], close[4:]
+    send_product(0, far + by_col + twin)
+    landed_one[gx] = product_one[gx]
     ends_one = ends_of(raw)
     peak_one = tallest(raw)
 
@@ -386,7 +388,10 @@
             pack_sides()
             send_sides(True)
 
-    send_product(product_two, landed_two, 1)
+    send_product(1, far)
+    send_product(0, by_row)
+    send_product(1, by_col + twin + by_row)
+    landed_two[gx] = product_two[gx]
     ends_two = ends_of(raw)
     outside = jnp.abs(row_lane // TILE * 2 - (RADIX - 1)) > RADIX // 2
     for dest in range(groups):

time: 29 us -> 29 us (level)
  no operation moved by 1% of the time
where the time goes in v6:
time: 29 us; the launch traced here: 28.8 us
  Pallas kernels  28.2 us (97%)
  between operations  0.64 us (2%)
    pallas_call x1, Pallas kernels, surface_by_kernel(): pl.pallas_call(functools.partial(surface_kernel, groups, columns), out_sh...  14.8 us
    pallas_call x1, Pallas kernels, write_all(): pl.pallas_call(write_kernel, in_specs=[vmem] * 4, out_specs=(hbm,) * 4, o...  13.4 us

profile of v6, /device:TPU:0, one launch (start us, length us, event | category | flops | bytes accessed | tf_op | source)
XLA Modules:
  0.0 28.8 jit_solution(1218835613153110387)
XLA Ops:
  0.6 14.8 %shard_map.84 = (f32[528,128]{1,0:T(8,128)S(1)}, f32[2,8,128]{2,1,0:T(8,128)S(1)}, f32[4,32,128]{2,1,0:T(8,128)S(1)}, f32[1,128]{1,0:T(1,128)S(1)}) custom-call(f32[2,256,128]{2,1,0:T(8,128)} %coef_hbm.1, f32[1,31]{1,0:T(1,128)} %bitcast.1, f32[2,32,31]{2,1,0:T(8,128)} %constant.6.clone.weights_hbm, bf16[512,512]{1,0:T(8,128)(2,1)} %constant.7.clone.basis_hbm, ...), custom_call_target="tpu_custom_call" | custom-call | tf_op jit(solution)/shard_map/pallas_call | solution.py:492
  15.5 13.4 %shard_map.85 = (f32[32,512,128]{2,1,0:T(8,128)}, f32[2,32,512,128]{3,2,1,0:T(8,128)}, f32[32,512,128]{2,1,0:T(8,128)}, f32[32,512,128]{2,1,0:T(8,128)}) custom-call(f32[528,128]{1,0:T(8,128)S(1)} %get-tuple-element.8.s_ref, f32[2,8,128]{2,1,0:T(8,128)S(1)} %get-tuple-element.9.sides, f32[4,32,128]{2,1,0:T(8,128)S(1)} %get-tuple-element.10.table, ...), custom_call_target="tpu_custom_call" | custom-call | tf_op jit(solution)/shard_map/pallas_call | solution.py:678
